TPU v7x, 32 devices: a whole 2x2x4 slice. The times are simulated.
32 devices in a mesh: row: 8 (over z, y), col: 4 (over x, core).
Axes of the slice: x: 2, y: 2, z: 4, core: 2. Of those that a mesh axis runs over, the one named last changes fastest.
Arguments:
- acts_in: bfloat16 [8192, 4608], P('row'), may hold values from -64 to 64
- grad_query: bfloat16 [8192, 4096], P('row', 'col'), may hold values from -2.828427 to 2.828427
- attn_out: bfloat16 [8192, 4096], P('row'), may hold values from -64 to 64
- grad_out: bfloat16 [8192, 4608], P('row', 'col'), may hold values from -2.828427 to 2.828427
- row_query: float32 [4608], P('row'), may hold values from 0.05 to 18
- col_query: float32 [4096], P('col'), may hold values from 0.05 to 2
- row_output: float32 [4096], P('row'), may hold values from 0.05 to 18
- col_output: float32 [4608], P('col'), may hold values from 0.05 to 2
Outputs:
- update_query: bfloat16 [4608, 4096], P('row', 'col')
- update_output: bfloat16 [4096, 4608], P('row', 'col')
- new_row_query: float32 [4608], P('row')
- new_col_query: float32 [4096], P('col')
- new_row_output: float32 [4096], P('row')
- new_col_output: float32 [4608], P('col')
All inputs are finite; a program needn't handle non-finite values.
Results may differ from a plain program's by a relative error of at most 0.028.
Values may be sent and summed in bfloat16 or wider, within the bound.
A program may use at most 128 MiB of HBM per device.

v0:
```python
import jax
import jax.numpy as jnp
from jax import lax
from jax.sharding import PartitionSpec as P

CLIP = 3072


decay_rate = 0.81
epsilon_one = 1e-30


def finish(
    gradient, clip_scale, row_old, col_old, row_sums, col_sums, row_level, whole_rows, whole_cols
):
    squared_scale = clip_scale * clip_scale
    row_new = decay_rate * row_old + (1.0 - decay_rate) * (
        squared_scale * row_sums / whole_cols + epsilon_one
    )
    col_new = decay_rate * col_old + (1.0 - decay_rate) * (
        squared_scale * col_sums / whole_rows + epsilon_one
    )
    update = clip_scale * gradient * lax.rsqrt(row_new[:, None] * col_new[None, :] / row_level)
    return (update.astype(jnp.bfloat16), row_new, col_new)


def shards(acts_in, grad_query, attn_out, grad_out, row_query, col_query, row_output, col_output):
    query_rows = row_query.shape[0]
    output_rows = row_output.shape[0]
    query_width = col_query.shape[0]
    output_width = col_output.shape[0]
    left_block = acts_in
    query_grad = lax.psum_scatter(
        lax.dot_general(
            left_block, grad_query, (((0,), (0,)), ((), ())), preferred_element_type=jnp.float32
        ).astype(jnp.bfloat16),
        "row",
        scatter_dimension=0,
        tiled=True,
    ).astype(jnp.float32)
    left_block = attn_out
    output_grad = lax.psum_scatter(
        lax.dot_general(
            left_block, grad_out, (((0,), (0,)), ((), ())), preferred_element_type=jnp.float32
        ).astype(jnp.bfloat16),
        "row",
        scatter_dimension=0,
        tiled=True,
    ).astype(jnp.float32)
    query_whole_rows = query_rows * lax.axis_size("row")
    output_whole_rows = output_rows * lax.axis_size("row")
    query_whole_cols = query_width * lax.axis_size("col")
    output_whole_cols = output_width * lax.axis_size("col")
    query_square = query_grad * query_grad
    output_square = output_grad * output_grad
    query_rowsum = jnp.sum(query_square, axis=1)
    output_rowsum = jnp.sum(output_square, axis=1)
    query_colsum = jnp.sum(query_square, axis=0)
    output_colsum = jnp.sum(output_square, axis=0)
    query_local = jnp.sum(query_rowsum)
    output_local = jnp.sum(output_rowsum)
    query_rowsum, output_rowsum, query_group, output_group = lax.psum(
        (query_rowsum, output_rowsum, query_local, output_local), "col"
    )
    query_colsum, output_colsum, query_squares, output_squares, query_oldsum, output_oldsum = (
        lax.psum(
            (
                query_colsum,
                output_colsum,
                query_group,
                output_group,
                jnp.sum(row_query),
                jnp.sum(row_output),
            ),
            "row",
        )
    )
    clip_scale = CLIP / jnp.maximum(jnp.sqrt(query_squares + output_squares), jnp.float32(CLIP))
    squared_scale = clip_scale * clip_scale
    query_level = decay_rate * query_oldsum / query_whole_rows + (1.0 - decay_rate) * (
        squared_scale * query_squares / (query_whole_rows * query_whole_cols) + epsilon_one
    )
    output_level = decay_rate * output_oldsum / output_whole_rows + (1.0 - decay_rate) * (
        squared_scale * output_squares / (output_whole_rows * output_whole_cols) + epsilon_one
    )
    update_query, new_row_query, new_col_query = finish(
        query_grad,
        clip_scale,
        row_query,
        col_query,
        query_rowsum,
        query_colsum,
        query_level,
        query_whole_rows,
        query_whole_cols,
    )
    update_output, new_row_output, new_col_output = finish(
        output_grad,
        clip_scale,
        row_output,
        col_output,
        output_rowsum,
        output_colsum,
        output_level,
        output_whole_rows,
        output_whole_cols,
    )
    return (
        update_query,
        update_output,
        new_row_query,
        new_col_query,
        new_row_output,
        new_col_output,
    )


def solution(mesh):
    in_specs = (
        P("row", None),
        P("row", "col"),
        P("row", None),
        P("row", "col"),
        P("row"),
        P("col"),
        P("row"),
        P("col"),
    )
    out_specs = (P("row", "col"), P("row", "col"), P("row"), P("col"), P("row"), P("col"))
    return jax.shard_map(shards, mesh=mesh, in_specs=in_specs, out_specs=out_specs, check_vma=False)
```

profile of v0, /device:TPU:0, one launch (start us, length us, event | category | flops | bytes accessed | tf_op | source)
XLA Modules:
  0.0 418.1 jit_solution(1630517620875365016)
XLA Ops:
  7.2 0.0 copy-start
  7.2 0.0 reduce-scatter.3.cloned.1.call-start
  7.2 16.7 %convolution_convert_fusion.1 = bf16[4608,1024]{1,0:T(8,128)(2,1)} fusion(bf16[1024,4608]{1,0:T(8,128)(2,1)} %param.8, bf16[1024,1024]{1,0:T(8,128)(2,1)} %param.9), kind=kOutput, calls=%fused_computation.1 | convolution fusion | flops 9668395008 | bytes 20971520 | tf_op jit(solution)/shard_map/dot_general | solution.py:34
  23.9 0.0 reduce-scatter.3.cloned.1.call-update
  23.9 0.2 reduce-scatter.5.cloned.1.call-start
  24.2 0.0 copy-done
  24.2 15.7 %convolution_convert_fusion = bf16[4096,1152]{1,0:T(8,128)(2,1)} fusion(bf16[1024,4096]{1,0:T(8,128)(2,1)} %param.10, bf16[1024,1152]{1,0:T(8,128)(2,1)S(1)} %copy-done), kind=kOutput, calls=%fused_computation | convolution fusion | flops 9668395008 | bytes 20185088 | tf_op jit(solution)/shard_map/dot_general | solution.py:43
  39.9 0.0 copy-start.5
  39.9 0.0 copy-start.7
  39.9 0.0 reduce-scatter.5.cloned.1.call-update
  39.9 0.7 copy-done.5
  40.6 0.6 reduce_sum.76
  41.2 0.0 copy-done.7
  41.2 0.7 reduce_sum.79
  41.9 147.1 %reduce-scatter.3.cloned.1.call-done = bf16[576,1024]{1,0:T(8,128)(2,1)} async-done(((bf16[4608,1024]{1,0:T(8,128)(2,1)}), bf16[576,1024]{1,0:T(8,128)(2,1)}) %reduce-scatter.3.cloned.1.call-update) | async-done | bytes 1179664 | tf_op jit(solution)/shard_map/reduce_scatter | solution.py:33
  188.9 2.6 fusion.4
  191.5 162.3 %reduce-scatter.5.cloned.1.call-done = bf16[512,1152]{1,0:T(8,128)(2,1)} async-done(((bf16[4096,1152]{1,0:T(8,128)(2,1)}), bf16[512,1152]{1,0:T(8,128)(2,1)}) %reduce-scatter.5.cloned.1.call-update) | async-done | bytes 1179664 | tf_op jit(solution)/shard_map/reduce_scatter | solution.py:42
  353.8 0.0 copy-start.1
  353.8 2.7 fusion.1
  356.5 7.2 %all-reduce.1 = (f32[]{:T(128)}, f32[]{:T(128)}, f32[576]{0:T(1024)}, f32[512]{0:T(512)}) all-reduce(f32[]{:T(128)} %get-tuple-element.11, f32[]{:T(128)} %get-tuple-element.8, f32[576]{0:T(1024)S(1)} %get-tuple-element.9, f32[512]{0:T(512)} %get-tuple-element.6), channel_id=1, replica_groups=mesh['row'=8,'col'=4] {'col'}, use_global_device_ids=true, to_apply=%region_2.0 | all-reduce | flops 1090 | bytes 8720 | tf_op jit(solution)/shard_map/psum | solution.py:62
  363.7 36.2 %all-reduce = (f32[]{:T(128)}, f32[]{:T(128)}, f32[]{:T(128)}, f32[1024]{0:T(1024)S(1)}, f32[]{:T(128)}, /*index=5*/f32[1152]{0:T(1024)}) all-reduce(f32[]{:T(128)} %reduce_sum.76, f32[]{:T(128)} %get-tuple-element.18, f32[]{:T(128)} %get-tuple-element.19, f32[1024]{0:T(1024)S(1)} %get-tuple-element.10, ...), channel_id=1, replica_groups=mesh['row'=8,'col'=4] {'row'}, use_global_device_ids=true, to_apply=%region_13.0 | all-reduce | flops 2180 | bytes 17440 | tf_op jit(solution)/shard_map/psum | solution.py:66
  402.5 0.7 multiply_add_fusion.2
  403.3 0.0 copy-start.3
  403.3 0.7 multiply_add_fusion.3
  404.0 0.0 copy-start.6
  404.7 0.7 multiply_add_fusion.1
  405.4 0.0 copy-start.4
  406.1 0.7 multiply_add_fusion
  406.8 0.0 copy-start.2
  406.8 2.8 fusion.7
  409.6 0.0 copy-done.1
  409.6 1.6 fusion.9
  411.2 0.0 copy-done.3
  411.2 0.0 copy-done.6
  411.2 0.0 copy-done.4
  411.2 0.0 copy-done.2
Async XLA Ops:
  7.2 17.0 %copy-start = (bf16[1024,1152]{1,0:T(8,128)(2,1)S(1)}, bf16[1024,1152]{1,0:T(8,128)(2,1)}, u32[]{:S(2)}) copy-start(bf16[1024,1152]{1,0:T(8,128)(2,1)} %param.11) | copy-start | bytes 7077892
  7.2 181.8 %reduce-scatter.3.cloned.1.call-start = ((), (), s32[]{:S(2)}) async-start(), calls=%async_computation.2 | async-start | bytes 10616832 | tf_op jit(solution)/shard_map/reduce_scatter | solution.py:33
  23.9 329.9 %reduce-scatter.5.cloned.1.call-start = ((), (), s32[]{:S(2)}) async-start(), calls=%async_computation.3 | async-start | bytes 10616832 | tf_op jit(solution)/shard_map/reduce_scatter | solution.py:42
  39.9 0.7 copy-start.5
  39.9 1.3 copy-start.7
  353.8 55.8 %copy-start.1 = (bf16[512,1152]{1,0:T(8,128)(2,1)S(1)}, bf16[512,1152]{1,0:T(8,128)(2,1)}, u32[]{:S(2)}) copy-start(bf16[512,1152]{1,0:T(8,128)(2,1)} %reduce-scatter.5.cloned.1.call-done) | copy-start | bytes 3538948
  403.3 7.9 %copy-start.3 = (f32[576]{0:T(1024)}, f32[576]{0:T(1024)S(1)}, u32[]{:S(2)}) copy-start(f32[576]{0:T(1024)S(1)} %multiply_add_fusion.2) | copy-start | bytes 6916
  404.0 7.2 %copy-start.6 = (f32[512]{0:T(512)}, f32[512]{0:T(512)S(1)}, u32[]{:S(2)}) copy-start(f32[512]{0:T(512)S(1)} %multiply_add_fusion.3) | copy-start | bytes 6148
  405.4 5.8 %copy-start.4 = (f32[1024]{0:T(1024)}, f32[1024]{0:T(1024)S(1)}, u32[]{:S(2)}) copy-start(f32[1024]{0:T(1024)S(1)} %multiply_add_fusion.1) | copy-start | bytes 12292
  406.8 4.4 %copy-start.2 = (f32[1152]{0:T(1024)}, f32[1152]{0:T(1024)S(1)}, u32[]{:S(2)}) copy-start(f32[1152]{0:T(1024)S(1)} %multiply_add_fusion) | copy-start | bytes 13828
Sparse Core Ops, SparseCore 0:
  24.1 164.8 reduce-scatter.2
  192.5 161.2 reduce-scatter.4
where the time goes:
time: 419 us; the launch traced here: 418 us
  waiting for transfers between devices  309 us (74%)
  blocking collectives  43.4 us (10%)
  matrix products  32.4 us (8%)
  between operations  18.2 us (4%)
  other arithmetic  13.8 us (3%)
    reduce_scatter x1, waiting for transfers between devices, shards(): lax.psum_scatter(lax.dot_general(left_block, grad_out, (((0,), (0,)), (()...  162 us
    reduce_scatter x1, waiting for transfers between devices, shards(): lax.psum_scatter(lax.dot_general(left_block, grad_query, (((0,), (0,)), (...  147 us
    psum x1, blocking collectives, shards(): lax.psum((query_colsum, output_colsum, query_group, output_group, jnp.sum...  36.2 us
    dot_general x1, matrix products, shards(): lax.dot_general(left_block, grad_query, (((0,), (0,)), ((), ())), preferr...  16.7 us
    dot_general x1, matrix products, shards(): lax.dot_general(left_block, grad_out, (((0,), (0,)), ((), ())), preferred...  15.7 us
  transfers between devices with their start and end apart: 2, of which 2 were waited for; matrix products, arithmetic and copies ran while one was open for 5% of the time, Pallas kernels for 0%

commit v1 on v0

v1 whole, which is shorter than its diff:
```python
import functools
import math

import jax
import jax.numpy as jnp
from jax import lax
from jax.experimental import pallas as pl
from jax.experimental.pallas import tpu as pltpu
from jax.sharding import PartitionSpec as P

CLIP = 3072
MESH = pl.DeviceIdType.MESH
LANES = 128

decay_rate = 0.81
epsilon_one = 1e-30


def round_up(value, step):
    return (value + step - 1) // step * step


class Plan:
    def __init__(self, total_rows, cols, n, tokens):
        self.rows = total_rows // n
        self.cols = cols
        self.tokens = tokens
        self.total_rows = total_rows
        self.window = round_up(self.rows + LANES - math.gcd(self.rows, LANES), LANES)
        tiles = cols // LANES
        self.width = LANES * max(t for t in (1, 2, 3) if tiles % t == 0)
        self.pieces = cols // self.width
        self.tile = max(t for t in (64, 48, 32, 16) if self.rows % t == 0)
        self.padded = round_up(self.rows, LANES)


def ring_row(pos, n):
    upper = pos // (n // 2)
    return (1 - upper) * (2 * pos) + upper * (2 * (n - 1 - pos) + 1)


def ring_pos(row, n):
    odd = row % 2
    return (1 - odd) * (row // 2) + odd * (n - 1 - row // 2)


def kernel(
    n, m, plans, lefts_q, rights_q, lefts_o, rights_o, vec_in,
    upd_q, upd_o, vec_out,
    right_q, right_o, win_q, win_o, lt_q, lt_o, part_q, part_o, first_q, first_o, ring_q, ring_o,
    rowacc_q, rowacc_o, packet1, inbox1, packet2, inbox2, scale_q, scale_o,
    load_sem, win_sem, send_q, recv_q, send_o, recv_o, psend1, precv1, psend2, precv2,
):
    row = lax.axis_index("row")
    col = lax.axis_index("col")
    pos = ring_pos(row, n)
    after = ring_row((pos + 1) % n, n)
    before = ring_row((pos + n - 1) % n, n)
    lefts = (lefts_q, lefts_o)
    rights = (right_q, right_o)
    wins = (win_q, win_o)
    lts = (lt_q, lt_o)
    parts = (part_q, part_o)
    firsts = (first_q, first_o)
    rings = (ring_q, ring_o)
    rowaccs = (rowacc_q, rowacc_o)
    scales = (scale_q, scale_o)
    upds = (upd_q, upd_o)
    sends = (send_q, send_o)
    recvs = (recv_q, recv_o)
    target = (after, before)

    loads = [
        pltpu.make_async_copy(rights_q, right_q, load_sem.at[0]),
        pltpu.make_async_copy(rights_o, right_o, load_sem.at[1]),
    ]

    def chunk_of(d, s):
        place = (pos - 1 - s + 2 * n) % n if d == 0 else (pos + 1 + s) % n
        return ring_row(place, n)

    def window_copy(d, s):
        plan = plans[d]
        start = chunk_of(d, s) * plan.rows // LANES * LANES
        return pltpu.make_async_copy(
            lefts[d].at[:, pl.ds(pl.multiple_of(start, LANES), plan.window)],
            wins[d].at[s % 2],
            win_sem.at[d, s % 2],
        )

    def offset_of(d, s):
        plan = plans[d]
        return pl.multiple_of(chunk_of(d, s) * plan.rows % LANES, math.gcd(plan.rows, LANES))

    def hop(d, k, s, src):
        return pltpu.make_async_remote_copy(
            src_ref=src,
            dst_ref=rings[d].at[s, k],
            send_sem=sends[d].at[s, k],
            recv_sem=recvs[d].at[s, k],
            device_id={"row": target[d]},
            device_id_type=MESH,
        )

    def turn(d, s):
        lts[d][...] = wins[d][s % 2].T

    def multiply(d, k):
        plan = plans[d]
        parts[d][k] = jnp.dot(
            lts[d][...],
            rights[d][:, pl.ds(k * plan.width, plan.width)],
            preferred_element_type=jnp.float32,
        )

    for d in range(2):
        loads[d].start()
        window_copy(d, 0).start()
    for d in range(2):
        window_copy(d, 1).start()

    barrier = pltpu.get_barrier_semaphore()
    for step in range(1, n):
        pl.semaphore_signal(barrier, inc=1, device_id={"row": (row + step) % n}, device_id_type=MESH)
    for step in range(1, m):
        pl.semaphore_signal(barrier, inc=1, device_id={"col": (col + step) % m}, device_id_type=MESH)

    def merge(d, k, s, add):
        plan = plans[d]
        off = offset_of(d, s)

        @pl.loop(0, plan.rows // plan.tile)
        def _(t):
            at = pl.multiple_of(t * plan.tile, plan.tile)
            own = parts[d][k, pl.ds(pl.multiple_of(off + at, 16), plan.tile), :]
            if add:
                own = own + rings[d][s - 1, k, pl.ds(at, plan.tile), :].astype(jnp.float32)
                rings[d][s - 1, k, pl.ds(at, plan.tile), :] = own.astype(jnp.bfloat16)
            else:
                firsts[d][k, pl.ds(at, plan.tile), :] = own.astype(jnp.bfloat16)

    order = sorted(
        [(k / plans[d].pieces, d, k) for d in range(2) for k in range(plans[d].pieces)]
    )
    order = [(d, k) for _, d, k in order]

    for d in range(2):
        loads[d].wait()
        window_copy(d, 0).wait()
        turn(d, 0)
    for i, (d, k) in enumerate(order):
        multiply(d, k)
        merge(d, k, 0, False)
        if i == 0:
            pl.semaphore_wait(barrier, n - 1 + m - 1)
        hop(d, k, 0, firsts[d].at[k]).start()

    @pl.loop(1, n - 1)
    def _(s):
        for d in range(2):
            window_copy(d, s).wait()
            turn(d, s)
            window_copy(d, s + 1).start()
            for k in range(plans[d].pieces):
                multiply(d, k)
        for d, k in order:
            hop(d, k, s - 1, rings[d].at[s - 1, k]).wait_recv()
            merge(d, k, s, True)
            hop(d, k, s, rings[d].at[s - 1, k]).start()

    last = n - 1
    for d in range(2):
        window_copy(d, last).wait()
        turn(d, last)
        for k in range(plans[d].pieces):
            multiply(d, k)

    width1 = plans[0].padded
    col_start = (0, plans[0].cols)
    for d in range(2):
        rowaccs[d][...] = jnp.zeros_like(rowaccs[d])
    for d, k in order:
        plan = plans[d]
        hop(d, k, last - 1, rings[d].at[last - 1, k]).wait_recv()
        off = offset_of(d, last)

        def gather(t, sums, d=d, k=k, plan=plan, off=off):
            at = pl.multiple_of(t * plan.tile, plan.tile)
            where = pl.ds(pl.multiple_of(off + at, 16), plan.tile)
            value = parts[d][k, where, :] + rings[d][last - 1, k, pl.ds(at, plan.tile), :].astype(
                jnp.float32
            )
            parts[d][k, where, :] = value
            square = value * value
            across = square[:, :LANES]
            for j in range(1, plan.width // LANES):
                across = across + square[:, j * LANES : (j + 1) * LANES]
            rowaccs[d][pl.ds(at, plan.tile), :] += across
            down = square[:8]
            for j in range(1, plan.tile // 8):
                down = down + square[j * 8 : (j + 1) * 8]
            return sums + down

        sums = lax.fori_loop(0, plan.rows // plan.tile, gather, jnp.zeros((8, plan.width), jnp.float32))
        packet2[:, pl.ds(col_start[d] + k * plan.width, plan.width)] = jnp.sum(
            sums, axis=0, keepdims=True
        )

    row_start = (0, width1)
    for d in range(2):
        packet1[:, pl.ds(row_start[d], plans[d].padded)] = jnp.sum(
            rowaccs[d][...].T, axis=0, keepdims=True
        )

    def share(axis, me, count, packet, inbox, ssem, rsem):
        copies = []
        for step in range(1, count):
            copies.append(
                pltpu.make_async_remote_copy(
                    src_ref=packet,
                    dst_ref=inbox.at[step - 1],
                    send_sem=ssem.at[step - 1],
                    recv_sem=rsem.at[step - 1],
                    device_id={axis: (me + step) % count},
                    device_id_type=MESH,
                )
            )
            copies[-1].start()
        total = packet[...]
        for step in range(1, count):
            copies[step - 1].wait_recv()
            total = total + inbox[step - 1]
        return total, copies

    row_total, copies1 = share("col", col, m, packet1, inbox1, psend1, precv1)
    row_sums = [row_total[:, row_start[d] : row_start[d] + plans[d].padded] for d in range(2)]
    row_old = [vec_in[:, pl.ds(row_start[d], plans[d].padded)] for d in range(2)]
    vec_col = width1 + plans[1].padded
    lane = lax.broadcasted_iota(jnp.int32, (1, LANES), 1)
    scalars = jnp.zeros((1, LANES), jnp.float32)
    for i, value in enumerate(row_sums + row_old):
        scalars = scalars + jnp.where(lane == i, jnp.sum(value, axis=1, keepdims=True), 0.0)
    all_cols = plans[0].cols + plans[1].cols
    packet2[:, pl.ds(all_cols, LANES)] = scalars
    col_total, copies2 = share("row", row, n, packet2, inbox2, psend2, precv2)
    tail = col_total[:, all_cols : all_cols + LANES]
    squares_q, squares_o, oldsum_q, oldsum_o = [
        jnp.sum(jnp.where(lane == i, tail, 0.0), axis=1, keepdims=True) for i in range(4)
    ]
    clip_scale = CLIP / jnp.maximum(jnp.sqrt(squares_q + squares_o), jnp.float32(CLIP))
    squared_scale = clip_scale * clip_scale
    squares = (squares_q, squares_o)
    oldsums = (oldsum_q, oldsum_o)
    for d in range(2):
        plan = plans[d]
        whole_cols = plan.cols * m
        level = decay_rate * oldsums[d] / plan.total_rows + (1.0 - decay_rate) * (
            squared_scale * squares[d] / (plan.total_rows * whole_cols) + epsilon_one
        )
        new_row = decay_rate * row_old[d] + (1.0 - decay_rate) * (
            squared_scale * row_sums[d] / whole_cols + epsilon_one
        )
        vec_out[:, pl.ds(row_start[d], plan.padded)] = new_row
        cols_at = pl.ds(vec_col + col_start[d], plan.cols)
        new_col = decay_rate * vec_in[:, cols_at] + (1.0 - decay_rate) * (
            squared_scale * col_total[:, col_start[d] : col_start[d] + plan.cols] / plan.total_rows
            + epsilon_one
        )
        vec_out[:, cols_at] = new_col
        across = clip_scale * lax.rsqrt(new_row / level)
        scales[d][...] = jnp.broadcast_to(across, (LANES, plan.padded)).T
        down = lax.rsqrt(new_col)
        off = offset_of(d, last)
        for k in range(plan.pieces):
            here = down[:, k * plan.width : (k + 1) * plan.width]

            @pl.loop(0, plan.rows // plan.tile)
            def _(t, d=d, k=k, plan=plan, off=off, here=here):
                at = pl.multiple_of(t * plan.tile, plan.tile)
                value = parts[d][k, pl.ds(pl.multiple_of(off + at, 16), plan.tile), :]
                factor = scales[d][pl.ds(at, plan.tile), :]
                factor = jnp.concatenate([factor] * (plan.width // LANES), axis=1)
                upds[d][pl.ds(at, plan.tile), pl.ds(k * plan.width, plan.width)] = (
                    value * factor * here
                ).astype(jnp.bfloat16)

    for copy in copies1 + copies2:
        copy.wait_send()

    for d, k in order:
        hop(d, k, 0, firsts[d].at[k]).wait_send()

    @pl.loop(1, n - 1)
    def _(s):
        for d, k in order:
            hop(d, k, s, rings[d].at[s - 1, k]).wait_send()


def shards(n, m, acts_in, grad_query, attn_out, grad_out, row_query, col_query, row_output, col_output):
    bf16, f32 = jnp.bfloat16, jnp.float32
    tokens = acts_in.shape[0]
    plans = (
        Plan(acts_in.shape[1], grad_query.shape[1], n, tokens),
        Plan(attn_out.shape[1], grad_out.shape[1], n, tokens),
    )
    a, b = plans
    vec = jnp.concatenate(
        [
            jnp.pad(row_query, (0, a.padded - a.rows)),
            jnp.pad(row_output, (0, b.padded - b.rows)),
            col_query,
            col_output,
        ]
    )[None, :]
    width = vec.shape[1]
    packet1 = a.padded + b.padded
    packet2 = a.cols + b.cols + LANES
    dma = pltpu.SemaphoreType.DMA
    vmem = pl.BlockSpec(memory_space=pltpu.VMEM)
    hbm = pl.BlockSpec(memory_space=pl.ANY)

    def each(make):
        return [make(a), make(b)]

    update_query, update_output, vec = pl.pallas_call(
        functools.partial(kernel, n, m, plans),
        out_shape=[
            jax.ShapeDtypeStruct((a.rows, a.cols), bf16),
            jax.ShapeDtypeStruct((b.rows, b.cols), bf16),
            jax.ShapeDtypeStruct((1, width), f32),
        ],
        in_specs=[hbm] * 4 + [vmem],
        out_specs=[vmem] * 3,
        scratch_shapes=[
            *each(lambda p: pltpu.VMEM((tokens, p.cols), bf16)),
            *each(lambda p: pltpu.VMEM((2, tokens, p.window), bf16)),
            *each(lambda p: pltpu.VMEM((p.window, tokens), bf16)),
            *each(lambda p: pltpu.VMEM((p.pieces, p.window, p.width), f32)),
            *each(lambda p: pltpu.VMEM((p.pieces, p.rows, p.width), bf16)),
            *each(lambda p: pltpu.VMEM((n - 1, p.pieces, p.rows, p.width), bf16)),
            *each(lambda p: pltpu.VMEM((p.padded, LANES), f32)),
            pltpu.VMEM((1, packet1), f32),
            pltpu.VMEM((m - 1, 1, packet1), f32),
            pltpu.VMEM((1, packet2), f32),
            pltpu.VMEM((n - 1, 1, packet2), f32),
            *each(lambda p: pltpu.VMEM((p.padded, LANES), f32)),
            dma((2,)),
            dma((2, 2)),
            dma((n - 1, a.pieces)),
            dma((n - 1, a.pieces)),
            dma((n - 1, b.pieces)),
            dma((n - 1, b.pieces)),
            dma((m - 1,)),
            dma((m - 1,)),
            dma((n - 1,)),
            dma((n - 1,)),
        ],
        compiler_params=pltpu.CompilerParams(
            collective_id=0, has_side_effects=True, vmem_limit_bytes=64000 * 1024
        ),
    )(acts_in, grad_query, attn_out, grad_out, vec)
    vec = vec[0]
    start = a.padded + b.padded
    return (
        update_query,
        update_output,
        vec[: a.rows],
        vec[start : start + a.cols],
        vec[a.padded : a.padded + b.rows],
        vec[start + a.cols :],
    )


def solution(mesh):
    in_specs = (
        P("row", None),
        P("row", "col"),
        P("row", None),
        P("row", "col"),
        P("row"),
        P("col"),
        P("row"),
        P("col"),
    )
    out_specs = (P("row", "col"), P("row", "col"), P("row"), P("col"), P("row"), P("col"))
    body = functools.partial(shards, mesh.shape["row"], mesh.shape["col"])
    return jax.shard_map(body, mesh=mesh, in_specs=in_specs, out_specs=out_specs, check_vma=False)
```

time: 419 us -> 210 us (0.50)
  waiting for transfers between devices: 309 us -> 0 us
  Pallas kernels: 0 us -> 199 us
  blocking collectives: 43.4 us -> 0 us
  matrix products: 32.4 us -> 0 us
  between operations: 18.2 us -> 0.65 us
  other arithmetic: 13.8 us -> 0.74 us
  local copies, waits for them, and re-layouts: 0.69 us -> 9.21 us
    reduce_scatter x2 -> x0, waiting for transfers between devices: 309 us -> none  [the longest x1 162 us: shards(): lax.psum_scatter(lax.dot_general(left_block, grad_out, (((0,), (0,)), (()...]
    pallas_call x0 -> x1, Pallas kernels: none -> 199 us  [shards(): pl.pallas_call(functools.partial(kernel, n, m, plans), out_shape=[jax.Sha...]
    psum x2 -> x0, blocking collectives: 43.4 us -> none  [the longest x1 36.2 us: shards(): lax.psum((query_colsum, output_colsum, query_group, output_group, jnp.sum...]
    dot_general x2 -> x0, matrix products: 32.4 us -> none  [the longest x1 16.7 us: shards(): lax.dot_general(left_block, grad_query, (((0,), (0,)), ((), ())), preferr...]
    reduce_sum x4 -> x0, other arithmetic: 6.55 us -> none  [the longest x1 2.67 us: shards(): output_rowsum = jnp.sum(output_square, axis=1)]
    slice x0 -> x4, local copies, waits for them, and re-layouts: none -> 5.21 us  [the longest x1 1.38 us: shards(): vec[:a.rows]]
    convert_element_type x2 -> x0, other arithmetic: 4.39 us -> none  [finish(): return (update.astype(jnp.bfloat16), row_new, col_new)]
  transfers between devices with their start and end apart: 2 -> 0, of which waited for: 2 -> 0; matrix products, arithmetic and copies ran while one was open for 5% -> 0% of each run, Pallas kernels for 0% -> 0%
where the time goes in v1:
time: 210 us
  Pallas kernels  199 us (95%)
  local copies, waits for them, and re-layouts  9.21 us (4%)
    pallas_call x1, Pallas kernels, shards(): pl.pallas_call(functools.partial(kernel, n, m, plans), out_shape=[jax.Sha...  199 us

profile of v1, /device:TPU:0, one launch (start us, length us, event | category | flops | bytes accessed | tf_op | source)
XLA Modules:
  0.0 210.1 jit_solution(14289570826505224989)
XLA Ops:
  0.6 0.7 fusion.1
  1.4 0.6 broadcast_in_dim.3.vec_in
  2.0 199.5 %shard_map.127 = (bf16[576,1024]{1,0:T(8,128)(2,1)}, bf16[512,1152]{1,0:T(8,128)(2,1)}, f32[1,3328]{1,0:T(1,128)}) custom-call(bf16[1024,4608]{1,0:T(8,128)(2,1)} %lefts_q.1, bf16[1024,1024]{1,0:T(8,128)(2,1)} %rights_q.1, bf16[1024,4096]{1,0:T(8,128)(2,1)} %lefts_o.1, bf16[1024,1152]{1,0:T(8,128)(2,1)} %rights_o.1, f32[1,3328]{1,0:T(1,128)} %broadcast_in_dim.3.vec_in), custom_call_target="tpu_custom_call" | custom-call | tf_op jit(solution)/shard_map/pallas_call | solution.py:325
  201.5 0.0 copy-start
  201.5 1.4 slice_reduce_fusion.1
  202.9 1.3 slice.26
  204.1 1.3 slice.28
  205.4 1.3 slice_reduce_fusion
  206.7 2.4 %copy.16 = bf16[576,1024]{1,0:T(8,128)(2,1)} copy(bf16[576,1024]{1,0:T(8,128)(2,1)} %get-tuple-element.18) | data formatting | bytes 2359296
  209.1 0.0 copy-done
  209.1 1.0 copy.17
Async XLA Ops:
  201.5 7.6 %copy-start = (bf16[512,1152]{1,0:T(8,128)(2,1)S(1)}, bf16[512,1152]{1,0:T(8,128)(2,1)}, u32[]{:S(2)}) copy-start(bf16[512,1152]{1,0:T(8,128)(2,1)} %get-tuple-element.19) | copy-start | bytes 3538948

commit v2 on v1

--- a/solution.py
+++ b/solution.py
@@ -32,6 +32,7 @@
         self.pieces = cols // self.width
         self.tile = max(t for t in (64, 48, 32, 16) if self.rows % t == 0)
         self.padded = round_up(self.rows, LANES)
+        self.parts = max(p for p in (1, 2, 3, 4) if self.rows % (16 * p) == 0)
 
 
 def ring_row(pos, n):
@@ -45,11 +46,11 @@
 
 
 def kernel(
-    n, m, plans, lefts_q, rights_q, lefts_o, rights_o, vec_in,
+    n, m, plans, lefts_q, rights_q, lefts_o, rights_o, old_row_q, old_row_o, old_col_q, old_col_o,
     upd_q, upd_o, vec_out,
     right_q, right_o, win_q, win_o, lt_q, lt_o, part_q, part_o, first_q, first_o, ring_q, ring_o,
-    rowacc_q, rowacc_o, packet1, inbox1, packet2, inbox2, scale_q, scale_o,
-    load_sem, win_sem, send_q, recv_q, send_o, recv_o, psend1, precv1, psend2, precv2,
+    rowacc_q, rowacc_o, packet1, inbox1, packet2, inbox2, packet3, inbox3, scale_q, scale_o,
+    load_sem, win_sem, send_q, recv_q, send_o, recv_o, psend1, precv1, psend2, precv2, psend3, precv3,
 ):
     row = lax.axis_index("row")
     col = lax.axis_index("col")
@@ -70,10 +71,12 @@
     recvs = (recv_q, recv_o)
     target = (after, before)
 
-    loads = [
-        pltpu.make_async_copy(rights_q, right_q, load_sem.at[0]),
-        pltpu.make_async_copy(rights_o, right_o, load_sem.at[1]),
-    ]
+    def load(d, k):
+        columns = pl.ds(k * plans[d].width, plans[d].width)
+        source = (rights_q, rights_o)[d]
+        return pltpu.make_async_copy(
+            source.at[:, columns], rights[d].at[:, columns], load_sem.at[d, k]
+        )
 
     def chunk_of(d, s):
         place = (pos - 1 - s + 2 * n) % n if d == 0 else (pos + 1 + s) % n
@@ -113,17 +116,20 @@
             preferred_element_type=jnp.float32,
         )
 
-    for d in range(2):
-        loads[d].start()
-        window_copy(d, 0).start()
-    for d in range(2):
-        window_copy(d, 1).start()
-
     barrier = pltpu.get_barrier_semaphore()
     for step in range(1, n):
         pl.semaphore_signal(barrier, inc=1, device_id={"row": (row + step) % n}, device_id_type=MESH)
     for step in range(1, m):
         pl.semaphore_signal(barrier, inc=1, device_id={"col": (col + step) % m}, device_id_type=MESH)
+
+    order = sorted(
+        [(k / plans[d].pieces, d, k) for d in range(2) for k in range(plans[d].pieces)]
+    )
+    order = [(d, k) for _, d, k in order]
+    for d, k in order:
+        if k == 0:
+            window_copy(d, 0).start()
+        load(d, k).start()
 
     def merge(d, k, s, add):
         plan = plans[d]
@@ -139,21 +145,18 @@
             else:
                 firsts[d][k, pl.ds(at, plan.tile), :] = own.astype(jnp.bfloat16)
 
-    order = sorted(
-        [(k / plans[d].pieces, d, k) for d in range(2) for k in range(plans[d].pieces)]
-    )
-    order = [(d, k) for _, d, k in order]
-
-    for d in range(2):
-        loads[d].wait()
-        window_copy(d, 0).wait()
-        turn(d, 0)
     for i, (d, k) in enumerate(order):
+        if k == 0:
+            window_copy(d, 0).wait()
+            turn(d, 0)
+        load(d, k).wait()
         multiply(d, k)
         merge(d, k, 0, False)
         if i == 0:
             pl.semaphore_wait(barrier, n - 1 + m - 1)
         hop(d, k, 0, firsts[d].at[k]).start()
+        if k == 0:
+            window_copy(d, 1).start()
 
     @pl.loop(1, n - 1)
     def _(s):
@@ -226,24 +229,32 @@
                 )
             )
             copies[-1].start()
+        return copies
+
+    def total_of(copies, packet, inbox):
         total = packet[...]
-        for step in range(1, count):
-            copies[step - 1].wait_recv()
-            total = total + inbox[step - 1]
-        return total, copies
-
-    row_total, copies1 = share("col", col, m, packet1, inbox1, psend1, precv1)
+        for i, copy in enumerate(copies):
+            copy.wait_recv()
+            total = total + inbox[i]
+        return total
+
+    copies1 = share("col", col, m, packet1, inbox1, psend1, precv1)
+    copies2 = share("row", row, n, packet2, inbox2, psend2, precv2)
+    row_total = total_of(copies1, packet1, inbox1)
     row_sums = [row_total[:, row_start[d] : row_start[d] + plans[d].padded] for d in range(2)]
-    row_old = [vec_in[:, pl.ds(row_start[d], plans[d].padded)] for d in range(2)]
+    row_old = [
+        jnp.pad(ref[...][None, :], ((0, 0), (0, plans[d].padded - plans[d].rows)))
+        for d, ref in enumerate((old_row_q, old_row_o))
+    ]
     vec_col = width1 + plans[1].padded
     lane = lax.broadcasted_iota(jnp.int32, (1, LANES), 1)
     scalars = jnp.zeros((1, LANES), jnp.float32)
     for i, value in enumerate(row_sums + row_old):
         scalars = scalars + jnp.where(lane == i, jnp.sum(value, axis=1, keepdims=True), 0.0)
-    all_cols = plans[0].cols + plans[1].cols
-    packet2[:, pl.ds(all_cols, LANES)] = scalars
-    col_total, copies2 = share("row", row, n, packet2, inbox2, psend2, precv2)
-    tail = col_total[:, all_cols : all_cols + LANES]
+    packet3[...] = scalars
+    copies3 = share("row", row, n, packet3, inbox3, psend3, precv3)
+    col_total = total_of(copies2, packet2, inbox2)
+    tail = total_of(copies3, packet3, inbox3)
     squares_q, squares_o, oldsum_q, oldsum_o = [
         jnp.sum(jnp.where(lane == i, tail, 0.0), axis=1, keepdims=True) for i in range(4)
     ]
@@ -262,7 +273,7 @@
         )
         vec_out[:, pl.ds(row_start[d], plan.padded)] = new_row
         cols_at = pl.ds(vec_col + col_start[d], plan.cols)
-        new_col = decay_rate * vec_in[:, cols_at] + (1.0 - decay_rate) * (
+        new_col = decay_rate * (old_col_q, old_col_o)[d][...][None, :] + (1.0 - decay_rate) * (
             squared_scale * col_total[:, col_start[d] : col_start[d] + plan.cols] / plan.total_rows
             + epsilon_one
         )
@@ -284,7 +295,7 @@
                     value * factor * here
                 ).astype(jnp.bfloat16)
 
-    for copy in copies1 + copies2:
+    for copy in copies1 + copies2 + copies3:
         copy.wait_send()
 
     for d, k in order:
@@ -294,6 +305,38 @@
     def _(s):
         for d, k in order:
             hop(d, k, s, rings[d].at[s - 1, k]).wait_send()
+
+
+def deliver(plans, in_q, in_o, vec, upd_q, upd_o, row_q, col_q, row_o, col_o, hold_q, hold_o, sem):
+    a, b = plans
+
+    def copy(d, i, out):
+        size = plans[d].rows // plans[d].parts
+        part = pl.ds(i * size, size)
+        hold = (hold_q, hold_o)[d].at[part]
+        source = (in_q, in_o)[d].at[part]
+        result = (upd_q, upd_o)[d].at[part]
+        if out:
+            return pltpu.make_async_copy(hold, result, sem.at[d, out, i])
+        return pltpu.make_async_copy(source, hold, sem.at[d, out, i])
+
+    every = [(d, i) for d in range(2) for i in range(plans[d].parts)]
+    for d, i in every:
+        copy(d, i, 0).start()
+    start = 0
+    for ref, size, padded in (
+        (row_q, a.rows, a.padded),
+        (row_o, b.rows, b.padded),
+        (col_q, a.cols, a.cols),
+        (col_o, b.cols, b.cols),
+    ):
+        ref[...] = vec[0, pl.ds(start, padded)][:size]
+        start += padded
+    for d, i in every:
+        copy(d, i, 0).wait()
+        copy(d, i, 1).start()
+    for d, i in every:
+        copy(d, i, 1).wait()
 
 
 def shards(n, m, acts_in, grad_query, attn_out, grad_out, row_query, col_query, row_output, col_output):
@@ -304,17 +347,10 @@
         Plan(attn_out.shape[1], grad_out.shape[1], n, tokens),
     )
     a, b = plans
-    vec = jnp.concatenate(
-        [
-            jnp.pad(row_query, (0, a.padded - a.rows)),
-            jnp.pad(row_output, (0, b.padded - b.rows)),
-            col_query,
-            col_output,
-        ]
-    )[None, :]
-    width = vec.shape[1]
+    olds = (row_query, row_output, col_query, col_output)
+    width = a.padded + b.padded + a.cols + b.cols
     packet1 = a.padded + b.padded
-    packet2 = a.cols + b.cols + LANES
+    packet2 = a.cols + b.cols
     dma = pltpu.SemaphoreType.DMA
     vmem = pl.BlockSpec(memory_space=pltpu.VMEM)
     hbm = pl.BlockSpec(memory_space=pl.ANY)
@@ -329,7 +365,7 @@
             jax.ShapeDtypeStruct((b.rows, b.cols), bf16),
             jax.ShapeDtypeStruct((1, width), f32),
         ],
-        in_specs=[hbm] * 4 + [vmem],
+        in_specs=[hbm] * 4 + [vmem] * 4,
         out_specs=[vmem] * 3,
         scratch_shapes=[
             *each(lambda p: pltpu.VMEM((tokens, p.cols), bf16)),
@@ -343,8 +379,10 @@
             pltpu.VMEM((m - 1, 1, packet1), f32),
             pltpu.VMEM((1, packet2), f32),
             pltpu.VMEM((n - 1, 1, packet2), f32),
+            pltpu.VMEM((1, LANES), f32),
+            pltpu.VMEM((n - 1, 1, LANES), f32),
             *each(lambda p: pltpu.VMEM((p.padded, LANES), f32)),
-            dma((2,)),
+            dma((2, max(a.pieces, b.pieces))),
             dma((2, 2)),
             dma((n - 1, a.pieces)),
             dma((n - 1, a.pieces)),
@@ -354,21 +392,30 @@
             dma((m - 1,)),
             dma((n - 1,)),
             dma((n - 1,)),
+            dma((n - 1,)),
+            dma((n - 1,)),
         ],
         compiler_params=pltpu.CompilerParams(
             collective_id=0, has_side_effects=True, vmem_limit_bytes=64000 * 1024
         ),
-    )(acts_in, grad_query, attn_out, grad_out, vec)
-    vec = vec[0]
-    start = a.padded + b.padded
-    return (
-        update_query,
-        update_output,
-        vec[: a.rows],
-        vec[start : start + a.cols],
-        vec[a.padded : a.padded + b.rows],
-        vec[start + a.cols :],
-    )
+    )(acts_in, grad_query, attn_out, grad_out, *olds)
+    return pl.pallas_call(
+        functools.partial(deliver, plans),
+        out_shape=[
+            jax.ShapeDtypeStruct((a.rows, a.cols), bf16),
+            jax.ShapeDtypeStruct((b.rows, b.cols), bf16),
+            jax.ShapeDtypeStruct((a.rows,), f32),
+            jax.ShapeDtypeStruct((a.cols,), f32),
+            jax.ShapeDtypeStruct((b.rows,), f32),
+            jax.ShapeDtypeStruct((b.cols,), f32),
+        ],
+        in_specs=[hbm, hbm, vmem],
+        out_specs=[hbm] * 2 + [vmem] * 4,
+        scratch_shapes=[
+            *each(lambda p: pltpu.VMEM((p.rows, p.cols), bf16)),
+            dma((2, 2, max(a.parts, b.parts))),
+        ],
+    )(update_query, update_output, vec)
 
 
 def solution(mesh):

time: 210 us -> 205 us (0.976)
  local copies, waits for them, and re-layouts: 9.21 us -> 0 us
  Pallas kernels: 199 us -> 204 us
    slice x4 -> x0, local copies, waits for them, and re-layouts: 5.21 us -> none  [the longest x1 1.38 us: shards(): vec[:a.rows]]
    pallas_call x0 -> x1, Pallas kernels: none -> 3.81 us  [shards(): pl.pallas_call(functools.partial(deliver, plans), out_shape=[jax.ShapeDty...]
    unnamed x4 -> x0, local copies, waits for them, and re-layouts: 3.38 us -> none
where the time goes in v2:
time: 205 us; the launch traced here: 204 us
  Pallas kernels  204 us (100%)
    pallas_call x1, Pallas kernels, shards(): pl.pallas_call(functools.partial(kernel, n, m, plans), out_shape=[jax.Sha...  200 us

profile of v2, /device:TPU:0, one launch (start us, length us, event | category | flops | bytes accessed | tf_op | source)
XLA Modules:
  0.0 204.3 jit_solution(11779937104160692805)
XLA Ops:
  0.6 199.9 %shard_map.127 = (bf16[576,1024]{1,0:T(8,128)(2,1)}, bf16[512,1152]{1,0:T(8,128)(2,1)}, f32[1,3328]{1,0:T(1,128)}) custom-call(bf16[1024,4608]{1,0:T(8,128)(2,1)} %lefts_q.1, bf16[1024,1024]{1,0:T(8,128)(2,1)} %rights_q.1, bf16[1024,4096]{1,0:T(8,128)(2,1)} %lefts_o.1, bf16[1024,1152]{1,0:T(8,128)(2,1)} %rights_o.1, f32[576]{0:T(1024)} %old_row_q.1, ...), custom_call_target="tpu_custom_call" | custom-call | tf_op jit(solution)/shard_map/pallas_call | solution.py:361
  200.5 3.8 %shard_map.128 = (bf16[576,1024]{1,0:T(8,128)(2,1)}, bf16[512,1152]{1,0:T(8,128)(2,1)}, f32[576]{0:T(1024)}, f32[1024]{0:T(1024)}, f32[512]{0:T(512)}, /*index=5*/f32[1152]{0:T(1024)}) custom-call(bf16[576,1024]{1,0:T(8,128)(2,1)} %get-tuple-element.9.in_q, bf16[512,1152]{1,0:T(8,128)(2,1)} %get-tuple-element.10.in_o, f32[1,3328]{1,0:T(1,128)} %get-tuple-element.11.vec), custom_call_target="tpu_custom_call" | custom-call | tf_op jit(solution)/shard_map/pallas_call | solution.py:402

commit v3 on v2

--- a/solution.py
+++ b/solution.py
@@ -47,10 +47,10 @@
 
 def kernel(
     n, m, plans, lefts_q, rights_q, lefts_o, rights_o, old_row_q, old_row_o, old_col_q, old_col_o,
-    upd_q, upd_o, vec_out,
+    grad_q, grad_o, vec_out, fac_out,
     right_q, right_o, win_q, win_o, lt_q, lt_o, part_q, part_o, first_q, first_o, ring_q, ring_o,
-    rowacc_q, rowacc_o, packet1, inbox1, packet2, inbox2, packet3, inbox3, scale_q, scale_o,
-    load_sem, win_sem, send_q, recv_q, send_o, recv_o, psend1, precv1, psend2, precv2, psend3, precv3,
+    rowacc_q, rowacc_o, packet1, inbox1, packet2, inbox2, packet3, inbox3,
+    load_sem, win_sem, out_sem, send_q, recv_q, send_o, recv_o, psend1, precv1, psend2, precv2, psend3, precv3,
 ):
     row = lax.axis_index("row")
     col = lax.axis_index("col")
@@ -65,8 +65,7 @@
     firsts = (first_q, first_o)
     rings = (ring_q, ring_o)
     rowaccs = (rowacc_q, rowacc_o)
-    scales = (scale_q, scale_o)
-    upds = (upd_q, upd_o)
+    grads = (grad_q, grad_o)
     sends = (send_q, send_o)
     recvs = (recv_q, recv_o)
     target = (after, before)
@@ -182,6 +181,15 @@
     col_start = (0, plans[0].cols)
     for d in range(2):
         rowaccs[d][...] = jnp.zeros_like(rowaccs[d])
+
+    def leave(d, k):
+        plan = plans[d]
+        return pltpu.make_async_copy(
+            parts[d].at[k, pl.ds(offset_of(d, last), plan.rows), :],
+            grads[d].at[:, pl.ds(k * plan.width, plan.width)],
+            out_sem.at[d, k],
+        )
+
     for d, k in order:
         plan = plans[d]
         hop(d, k, last - 1, rings[d].at[last - 1, k]).wait_recv()
@@ -208,6 +216,7 @@
         packet2[:, pl.ds(col_start[d] + k * plan.width, plan.width)] = jnp.sum(
             sums, axis=0, keepdims=True
         )
+        leave(d, k).start()
 
     row_start = (0, width1)
     for d in range(2):
@@ -278,23 +287,11 @@
             + epsilon_one
         )
         vec_out[:, cols_at] = new_col
-        across = clip_scale * lax.rsqrt(new_row / level)
-        scales[d][...] = jnp.broadcast_to(across, (LANES, plan.padded)).T
-        down = lax.rsqrt(new_col)
-        off = offset_of(d, last)
-        for k in range(plan.pieces):
-            here = down[:, k * plan.width : (k + 1) * plan.width]
-
-            @pl.loop(0, plan.rows // plan.tile)
-            def _(t, d=d, k=k, plan=plan, off=off, here=here):
-                at = pl.multiple_of(t * plan.tile, plan.tile)
-                value = parts[d][k, pl.ds(pl.multiple_of(off + at, 16), plan.tile), :]
-                factor = scales[d][pl.ds(at, plan.tile), :]
-                factor = jnp.concatenate([factor] * (plan.width // LANES), axis=1)
-                upds[d][pl.ds(at, plan.tile), pl.ds(k * plan.width, plan.width)] = (
-                    value * factor * here
-                ).astype(jnp.bfloat16)
-
+        fac_out[:, pl.ds(row_start[d], plan.padded)] = clip_scale * lax.rsqrt(new_row / level)
+        fac_out[:, cols_at] = lax.rsqrt(new_col)
+
+    for d, k in order:
+        leave(d, k).wait()
     for copy in copies1 + copies2 + copies3:
         copy.wait_send()
 
@@ -307,18 +304,22 @@
             hop(d, k, s, rings[d].at[s - 1, k]).wait_send()
 
 
-def deliver(plans, in_q, in_o, vec, upd_q, upd_o, row_q, col_q, row_o, col_o, hold_q, hold_o, sem):
+def deliver(
+    plans, in_q, in_o, vec, factors, upd_q, upd_o, row_q, col_q, row_o, col_o,
+    grad_q, grad_o, hold_q, hold_o, scale_q, scale_o, sem,
+):
     a, b = plans
 
     def copy(d, i, out):
         size = plans[d].rows // plans[d].parts
         part = pl.ds(i * size, size)
-        hold = (hold_q, hold_o)[d].at[part]
-        source = (in_q, in_o)[d].at[part]
-        result = (upd_q, upd_o)[d].at[part]
         if out:
-            return pltpu.make_async_copy(hold, result, sem.at[d, out, i])
-        return pltpu.make_async_copy(source, hold, sem.at[d, out, i])
+            return pltpu.make_async_copy(
+                (hold_q, hold_o)[d].at[part], (upd_q, upd_o)[d].at[part], sem.at[d, out, i]
+            )
+        return pltpu.make_async_copy(
+            (in_q, in_o)[d].at[part], (grad_q, grad_o)[d].at[part], sem.at[d, out, i]
+        )
 
     every = [(d, i) for d in range(2) for i in range(plans[d].parts)]
     for d, i in every:
@@ -332,8 +333,27 @@
     ):
         ref[...] = vec[0, pl.ds(start, padded)][:size]
         start += padded
+    row_start = (0, a.padded)
+    col_start = (a.padded + b.padded, a.padded + b.padded + a.cols)
+    scales = (scale_q, scale_o)
+    for d in range(2):
+        across = factors[:, pl.ds(row_start[d], plans[d].padded)]
+        scales[d][...] = jnp.broadcast_to(across, (LANES, plans[d].padded)).T
     for d, i in every:
+        plan = plans[d]
+        size = plan.rows // plan.parts
+        grad, hold = (grad_q, grad_o)[d], (hold_q, hold_o)[d]
         copy(d, i, 0).wait()
+
+        @pl.loop(0, size // 16)
+        def _(t, d=d, i=i, plan=plan, size=size, grad=grad, hold=hold):
+            rows = pl.ds(pl.multiple_of(i * size + t * 16, 16), 16)
+            factor = scales[d][rows, :]
+            for j in range(plan.cols // LANES):
+                lanes = pl.ds(j * LANES, LANES)
+                down = factors[:, pl.ds(col_start[d] + j * LANES, LANES)]
+                hold[rows, lanes] = (grad[rows, lanes] * factor * down).astype(jnp.bfloat16)
+
         copy(d, i, 1).start()
     for d, i in every:
         copy(d, i, 1).wait()
@@ -358,15 +378,16 @@
     def each(make):
         return [make(a), make(b)]
 
-    update_query, update_output, vec = pl.pallas_call(
+    query_grad, output_grad, vec, factors = pl.pallas_call(
         functools.partial(kernel, n, m, plans),
         out_shape=[
-            jax.ShapeDtypeStruct((a.rows, a.cols), bf16),
-            jax.ShapeDtypeStruct((b.rows, b.cols), bf16),
+            jax.ShapeDtypeStruct((a.rows, a.cols), f32),
+            jax.ShapeDtypeStruct((b.rows, b.cols), f32),
+            jax.ShapeDtypeStruct((1, width), f32),
             jax.ShapeDtypeStruct((1, width), f32),
         ],
         in_specs=[hbm] * 4 + [vmem] * 4,
-        out_specs=[vmem] * 3,
+        out_specs=[hbm] * 2 + [vmem] * 2,
         scratch_shapes=[
             *each(lambda p: pltpu.VMEM((tokens, p.cols), bf16)),
             *each(lambda p: pltpu.VMEM((2, tokens, p.window), bf16)),
@@ -381,9 +402,9 @@
             pltpu.VMEM((n - 1, 1, packet2), f32),
             pltpu.VMEM((1, LANES), f32),
             pltpu.VMEM((n - 1, 1, LANES), f32),
-            *each(lambda p: pltpu.VMEM((p.padded, LANES), f32)),
             dma((2, max(a.pieces, b.pieces))),
             dma((2, 2)),
+            dma((2, max(a.pieces, b.pieces))),
             dma((n - 1, a.pieces)),
             dma((n - 1, a.pieces)),
             dma((n - 1, b.pieces)),
@@ -409,13 +430,15 @@
             jax.ShapeDtypeStruct((b.rows,), f32),
             jax.ShapeDtypeStruct((b.cols,), f32),
         ],
-        in_specs=[hbm, hbm, vmem],
+        in_specs=[hbm, hbm, vmem, vmem],
         out_specs=[hbm] * 2 + [vmem] * 4,
         scratch_shapes=[
+            *each(lambda p: pltpu.VMEM((p.rows, p.cols), f32)),
             *each(lambda p: pltpu.VMEM((p.rows, p.cols), bf16)),
+            *each(lambda p: pltpu.VMEM((p.padded, LANES), f32)),
             dma((2, 2, max(a.parts, b.parts))),
         ],
-    )(update_query, update_output, vec)
+    )(query_grad, output_grad, vec, factors)
 
 
 def solution(mesh):

time: 205 us -> 204 us (level)
  no operation moved by 1% of the time
where the time goes in v3:
time: 204 us
  Pallas kernels  203 us (100%)
    pallas_call x1, Pallas kernels, shards(): pl.pallas_call(functools.partial(kernel, n, m, plans), out_shape=[jax.Sha...  198 us
    pallas_call x1, Pallas kernels, shards(): pl.pallas_call(functools.partial(deliver, plans), out_shape=[jax.ShapeDty...  4.98 us

profile of v3, /device:TPU:0, one launch (start us, length us, event | category | flops | bytes accessed | tf_op | source)
XLA Modules:
  0.0 203.6 jit_solution(5926582826183676305)
XLA Ops:
  0.6 197.9 %shard_map.127 = (f32[576,1024]{1,0:T(8,128)}, f32[512,1152]{1,0:T(8,128)}, f32[1,3328]{1,0:T(1,128)}, f32[1,3328]{1,0:T(1,128)}) custom-call(bf16[1024,4608]{1,0:T(8,128)(2,1)} %lefts_q.1, bf16[1024,1024]{1,0:T(8,128)(2,1)} %rights_q.1, bf16[1024,4096]{1,0:T(8,128)(2,1)} %lefts_o.1, bf16[1024,1152]{1,0:T(8,128)(2,1)} %rights_o.1, f32[576]{0:T(1024)} %old_row_q.1, ...), custom_call_target="tpu_custom_call" | custom-call | tf_op jit(solution)/shard_map/pallas_call | solution.py:381
  198.6 5.0 %shard_map.128 = (bf16[576,1024]{1,0:T(8,128)(2,1)}, bf16[512,1152]{1,0:T(8,128)(2,1)}, f32[576]{0:T(1024)}, f32[1024]{0:T(1024)}, f32[512]{0:T(512)}, /*index=5*/f32[1152]{0:T(1024)}) custom-call(f32[576,1024]{1,0:T(8,128)} %get-tuple-element.10.in_q, f32[512,1152]{1,0:T(8,128)} %get-tuple-element.11.in_o, f32[1,3328]{1,0:T(1,128)} %get-tuple-element.12.vec, ...), custom_call_target="tpu_custom_call" | custom-call | tf_op jit(solution)/shard_map/pallas_call | solution.py:423
